TPU v7x, 256 devices: a whole 4x4x8 slice. The times are simulated.
256 devices in a mesh: row: 8 (over z_hi, core), sa: 32 (over z_lo, x, y).
Axes of the slice: x: 4, y: 4, z: 8 (z_hi: 4, z_lo: 2; z = z_hi * 2 + z_lo), core: 2. Of those that a mesh axis runs over, the one named last changes fastest.
Arguments:
- rep_w1: float32 [16, 8, 128, 4096], P('row', None, None, 'sa'), may hold values from -6 to 6
- rep_w3: float32 [16, 8, 128, 4096], P('row', None, None, 'sa'), may hold values from -6 to 6
- rep_w2: float32 [16, 8, 128, 4096], P('row', None, None, 'sa'), may hold values from -6 to 6
- rep_gate: float32 [16, 8, 4096], P('row', None, 'sa'), may hold values from -6 to 6
Outputs:
- serve_w1: bfloat16 [8, 128, 4096], P('row', 'sa')
- serve_w3: bfloat16 [8, 128, 4096], P('row', 'sa')
- serve_w2: bfloat16 [8, 128, 4096], P('row', 'sa')
- serve_gate: bfloat16 [8, 4096], replicated
- soup_norms: float32 [8, 4], P('row')
- replica_norms: float32 [16, 8, 4], P('row')
All inputs are finite; a program needn't handle non-finite values.
Results may differ from a plain program's by a relative error of at most 0.001.
Values may be sent and summed in bfloat16 or wider, within the bound.
A program may use at most 64 MiB of HBM per device.

v0:
```python
import functools

import jax
import jax.numpy as jnp
from jax import lax
from jax.sharding import Mesh
from jax.sharding import PartitionSpec as P

SA = ("sa_0", "sa_1", "sa_2")


def own_rows_2(product, width, axis):
    everything = product(jnp.int32(0), lax.axis_size(axis) * width)
    own = lax.psum_scatter(everything, axis, scatter_dimension=0, tiled=True)
    return own


def padded_to(lines, count):
    spare = -lines.shape[0] % count
    if not spare:
        return lines
    return jnp.concatenate([lines, jnp.zeros((spare, *lines.shape[1:]), lines.dtype)])


def sum_by_parts(array, axis):
    lines = array.reshape(-1, *array.shape[1:][-1:])
    own = lax.psum_scatter(
        padded_to(lines, lax.axis_size(axis)), axis, scatter_dimension=0, tiled=True
    )
    whole = lax.all_gather(own, axis).reshape(-1, *lines.shape[1:])
    return lax.slice_in_dim(whole, 0, len(lines)).reshape(array.shape)


def laid_out(blocks, dim):
    blocks = jnp.moveaxis(blocks, 0, dim)
    shape = blocks.shape
    return blocks.reshape(*shape[:dim], shape[dim] * shape[dim + 1], *shape[dim + 2 :])


def stacked_from(array, axes, order):
    blocks = array
    for k in order:
        blocks = lax.all_gather(blocks, axes[k])
    done = order[::-1]
    back = [done.index(k) for k in range(len(axes))]
    blocks = blocks.transpose(*back, *range(len(axes), blocks.ndim))
    return blocks.reshape(-1, *array.shape)


def gather_axes(array, axes, order, dim):
    return laid_out(stacked_from(array, axes, order), dim)


def by_axis(array, axes):
    return functools.reduce(lax.psum, axes, array)


def square_sums(values, dims_summed):
    return jnp.sum(values * values, axis=dims_summed)


def body(rep_w1, rep_w3, rep_w2, rep_gate):
    rows_total = lax.axis_size("row")
    replicas = rep_w1.shape[0] * rows_total
    experts_all = rep_w1.shape[1]
    expert_rows = experts_all // rows_total
    hidden_all = rep_w1.shape[2]
    model_width = rep_w1.shape[3] * lax.axis_size(SA)
    weights = (rep_w1, rep_w3, rep_w2)
    replica_parts = jnp.stack(
        [square_sums(weight, (2, 3)) for weight in weights] + [square_sums(rep_gate, 2)], axis=2
    )

    def expert_terms(offset, length):
        pieces = [
            jnp.sum(lax.dynamic_slice_in_dim(weight, offset, length, 1), axis=0)
            for weight in weights
        ]
        return jnp.stack(pieces, axis=1)

    summed = own_rows_2(expert_terms, expert_rows, "row")
    served = (summed / replicas).astype(jnp.bfloat16)
    arranged = lax.all_to_all(served, SA, split_axis=2, concat_axis=3, tiled=True)
    served_list = [arranged[:, column] for column in range(3)]
    gate_local = jnp.sum(rep_gate, axis=0)
    gate_total = sum_by_parts(gate_local, "row")
    gate_shard = (gate_total / replicas).astype(jnp.bfloat16)
    serve_gate = gather_axes(gate_shard, SA, (0, 1, 2), 1)
    own_rows = lax.dynamic_slice_in_dim(
        gate_shard, lax.axis_index("row") * expert_rows, expert_rows, 0
    )
    soup_parts = jnp.stack(
        [square_sums(served.astype(jnp.float32), (1, 2)) for served in served_list]
        + [square_sums(own_rows.astype(jnp.float32), 1)],
        axis=1,
    )
    replica_total, soup_total = (by_axis(replica_parts, SA), by_axis(soup_parts, SA))
    counts = jnp.array([hidden_all * model_width] * 3 + [model_width], jnp.float32)
    replica_norms = jnp.sqrt(replica_total / counts)
    soup_norms = jnp.sqrt(soup_total / counts)
    return (served_list[0], served_list[1], served_list[2], serve_gate, soup_norms, replica_norms)


def solution(mesh):
    torus = Mesh(mesh.devices.reshape(mesh.shape["row"], 2, 4, 4), ("row", "sa_0", "sa_1", "sa_2"))
    in_specs = (
        P("row", None, None, SA),
        P("row", None, None, SA),
        P("row", None, None, SA),
        P("row", None, SA),
    )
    out_specs = (
        P("row", SA, None),
        P("row", SA, None),
        P("row", SA, None),
        P(),
        P("row", None),
        P("row", None, None),
    )
    return jax.shard_map(body, mesh=torus, in_specs=in_specs, out_specs=out_specs, check_vma=False)
```

profile of v0, /device:TPU:2, one launch (start us, length us, event | category | flops | bytes accessed | tf_op | source)
XLA Modules:
  0.0 130.5 jit_solution(17366467188099708653)
XLA Ops:
  7.2 0.0 copy-start
  7.2 0.0 reduce-scatter.2.cloned.1.call-start
  7.2 1.6 %multiply_reduce_fusion.2 = (f32[2,8]{1,0:T(2,128)S(1)}, f32[8,128,128]{2,1,0:T(8,128)S(1)}) fusion(f32[2,8,128,128]{3,2,1,0:T(8,128)} %param.5), kind=kLoop, calls=%fused_computation.3 | loop fusion | flops 655344 | bytes 1572928 | tf_op jit(solution)/shard_map/reduce_sum | solution.py:59
  8.8 1.6 %multiply_reduce_fusion = (f32[2,8]{1,0:T(2,128)S(1)}, f32[8,128,128]{2,1,0:T(8,128)S(1)}, f32[8,128,128]{2,1,0:T(8,128)S(1)}, f32[2,8]{1,0:T(2,128)S(1)}) fusion(f32[2,8,128,128]{3,2,1,0:T(8,128)S(1)} %copy-done, f32[2,8,128,128]{3,2,1,0:T(8,128)} %param.6), kind=kLoop, calls=%fused_computation.1 | loop fusion | flops 1310688 | bytes 3145856 | tf_op jit(solution)/shard_map/reduce_sum | solution.py:59
  10.4 0.1 pad_maximum_fusion
  10.5 1.3 copy.25
  11.8 0.0 reduce-scatter.2.cloned.1.call-update
  11.8 0.6 copy-done.3
  12.5 0.6 dynamic-slice.3
  13.1 0.0 copy-done.1
  13.1 0.1 multiply_reduce_fusion.6
  13.1 20.5 %all-reduce = f32[8,128]{1,0:T(8,128)S(1)} all-reduce(f32[8,128]{1,0:T(8,128)S(1)} %get-tuple-element.49), channel_id=8, replica_groups=mesh['row'=8,'sa_0'=2,'sa_1'=4,'sa_2'=4] {'row'}, use_global_device_ids=true, to_apply=%region_5.0.clone | all-reduce | flops 1024 | bytes 8192
  33.6 0.6 dynamic-slice_bitcast_fusion
  34.3 8.8 %all-gather.5 = f32[8,1,128]{2,1,0:T(1,128)S(1)} all-gather(f32[1,1,128]{2,1,0:T(1,128)S(1)} %dynamic-slice_bitcast_fusion), channel_id=2, replica_groups=mesh['row'=8,'sa_0'=2,'sa_1'=4,'sa_2'=4] {'row'}, dimensions={0}, use_global_device_ids=true | all-gather | bytes 4608 | tf_op jit(solution)/shard_map/all_gather | solution.py:30
  43.0 13.2 %reduce-scatter.2.cloned.1.call-done = f32[1,3,128,128]{3,2,1,0:T(8,128)} async-done(((f32[8,3,128,128]{3,2,1,0:T(8,128)}), f32[1,3,128,128]{3,2,1,0:T(8,128)}) %reduce-scatter.2.cloned.1.call-update) | async-done | bytes 196624 | tf_op jit(solution)/shard_map/reduce_scatter | solution.py:14
  56.3 0.9 multiply_convert_fusion
  57.2 0.7 copy.26
  57.9 7.2 %all-to-all-start = ((bf16[1,3,128,128]{3,1,0,2:T(4,128)(2,1)}), bf16[1,3,128,128]{3,1,0,2:T(4,128)(2,1)S(1)}, u32[]{:S(2)}, u32[]{:S(2)}) async-start(bf16[1,3,128,128]{3,1,0,2:T(4,128)(2,1)} %copy.26), calls=%async_computation.1 | async-start | bytes 262144 | tf_op jit(solution)/shard_map/all_to_all | solution.py:83
  65.1 0.6 multiply_reduce_fusion.7
  65.7 4.3 %all-gather.4 = bf16[16,128]{1,0:T(8,128)(2,1)S(1)} all-gather(bf16[8,128]{1,0:T(8,128)(2,1)S(1)} %fusion), channel_id=6, replica_groups=mesh['row'=8,'sa_0'=2,'sa_1'=4,'sa_2'=4] {'sa_0'}, dimensions={0}, use_global_device_ids=true | all-gather | bytes 6144 | tf_op jit(solution)/shard_map/all_gather | solution.py:43
  70.1 11.8 %all-gather.2 = bf16[8,8,128]{2,1,0:T(8,128)(2,1)S(1)} all-gather(bf16[2,8,128]{2,1,0:T(8,128)(2,1)S(1)} %bitcast.50), channel_id=4, replica_groups=mesh['row'=8,'sa_0'=2,'sa_1'=4,'sa_2'=4] {'sa_1'}, dimensions={0}, use_global_device_ids=true | all-gather | bytes 20480 | tf_op jit(solution)/shard_map/all_gather | solution.py:43
  81.9 12.1 %all-gather.3 = bf16[16,2,8,128]{3,2,1,0:T(8,128)(2,1)S(1)} all-gather(bf16[4,2,8,128]{3,2,1,0:T(8,128)(2,1)S(1)} %bitcast.46), channel_id=5, replica_groups=mesh['row'=8,'sa_0'=2,'sa_1'=4,'sa_2'=4] {'sa_2'}, dimensions={0}, use_global_device_ids=true | all-gather | bytes 81920 | tf_op jit(solution)/shard_map/all_gather | solution.py:43
  94.0 0.0 all-to-all-done
  94.1 1.3 multiply_reduce_fusion.3
  95.4 2.6 %pad_maximum_fusion.2 = f32[1,4]{1,0:T(1,128)S(1)} fusion(f32[1,1]{1,0:T(1,128)} %bitcast.25, f32[1,1]{1,0:T(1,128)} %bitcast.24, f32[1,1]{1,0:T(1,128)} %bitcast.23, f32[1,1]{1,0:T(1,128)} %bitcast.22), kind=kLoop, calls=%fused_computation.15 | loop fusion | flops 12 | bytes 32 | tf_op jit(solution)/shard_map/stack | solution.py:92
  97.9 0.6 copy.29
  98.6 5.0 %all-reduce.3 = (f32[1,4]{1,0:T(1,128)S(1)}, f32[2,8,4]{1,0,2:T(2,128)S(1)}) all-reduce(f32[1,4]{1,0:T(1,128)S(1)} %pad_maximum_fusion.2, f32[2,8,4]{1,0,2:T(2,128)S(1)} %pad_maximum_fusion.1), channel_id=1, replica_groups=mesh['row'=8,'sa_0'=2,'sa_1'=4,'sa_2'=4] {'sa_0'}, use_global_device_ids=true, to_apply=%region_10.0 | all-reduce | flops 68 | bytes 544 | tf_op jit(solution)/shard_map/psum | solution.py:55
  103.5 8.7 %all-reduce.2 = (f32[1,4]{1,0:T(1,128)S(1)}, f32[2,8,4]{1,0,2:T(2,128)S(1)}) all-reduce(f32[1,4]{1,0:T(1,128)S(1)} %get-tuple-element.54, f32[2,8,4]{1,0,2:T(2,128)S(1)} %get-tuple-element.55), channel_id=1, replica_groups=mesh['row'=8,'sa_0'=2,'sa_1'=4,'sa_2'=4] {'sa_1'}, use_global_device_ids=true, to_apply=%region_11.0 | all-reduce | flops 68 | bytes 544 | tf_op jit(solution)/shard_map/psum | solution.py:55
  112.2 10.2 %all-reduce.1 = (f32[1,4]{1,0:T(1,128)S(1)}, f32[2,8,4]{1,0,2:T(2,128)S(1)}) all-reduce(f32[1,4]{1,0:T(1,128)S(1)} %get-tuple-element.52, f32[2,8,4]{1,0,2:T(2,128)S(1)} %get-tuple-element.53), channel_id=1, replica_groups=mesh['row'=8,'sa_0'=2,'sa_1'=4,'sa_2'=4] {'sa_2'}, use_global_device_ids=true, to_apply=%region_12.0 | all-reduce | flops 68 | bytes 544 | tf_op jit(solution)/shard_map/psum | solution.py:55
  122.4 0.1 multiply_sqrt_fusion
  122.5 0.6 copy.30
  123.1 0.5 multiply_sqrt_fusion.1
  (11 shorter events, 0.0 us)
Async XLA Ops:
  7.2 1.6 %copy-start = (f32[2,8,128,128]{3,2,1,0:T(8,128)S(1)}, f32[2,8,128,128]{3,2,1,0:T(8,128)}, u32[]{:S(2)}) copy-start(f32[2,8,128,128]{3,2,1,0:T(8,128)} %param.7) | copy-start | bytes 3145732
  7.2 49.1 %reduce-scatter.2.cloned.1.call-start = ((), (), s32[]{:S(2)}) async-start(), calls=%async_computation.2 | async-start | bytes 1769472 | tf_op jit(solution)/shard_map/reduce_scatter | solution.py:14
  11.8 0.7 copy-start.3
  11.8 1.3 copy-start.1
  11.8 110.6 %copy-start.2 = (f32[4]{0:T(128)S(1)}, f32[4]{0:T(128)}, u32[]{:S(2)}) copy-start(f32[4]{0:T(128)} %constant.25) | copy-start | bytes 52
  11.8 111.3 %copy-start.4 = (f32[1,4]{1,0:T(1,128)S(1)}, f32[1,4]{1,0:T(1,128)}, u32[]{:S(2)}) copy-start(f32[1,4]{1,0:T(1,128)} %constant.27) | copy-start | bytes 52
  57.9 36.1 %all-to-all-start = ((bf16[1,3,128,128]{3,1,0,2:T(4,128)(2,1)}), bf16[1,3,128,128]{3,1,0,2:T(4,128)(2,1)S(1)}, u32[]{:S(2)}, u32[]{:S(2)}) async-start(bf16[1,3,128,128]{3,1,0,2:T(4,128)(2,1)} %copy.26), calls=%async_computation.1 | async-start | bytes 262144 | tf_op jit(solution)/shard_map/all_to_all | solution.py:83
Sparse Core Ops, SparseCore 0:
  11.9 44.2 reduce-scatter.1
where the time goes:
time: 132 us; the launch traced here: 130 us
  blocking collectives  81.3 us (62%)
  between operations  14.1 us (11%)
  waiting for transfers between devices  13.2 us (10%)
  other arithmetic  9.41 us (7%)
  starting transfers between devices  7.23 us (5%)
  local copies, waits for them, and re-layouts  5.13 us (4%)
    all_gather x3, blocking collectives, stacked_from(): blocks = lax.all_gather(blocks, axes[k])  28.3 us
    psum x3, blocking collectives, by_axis(): return functools.reduce(lax.psum, axes, array)  23.8 us
    unnamed x1, blocking collectives  20.5 us
    reduce_scatter x1, waiting for transfers between devices, own_rows_2(): own = lax.psum_scatter(everything, axis, scatter_dimension=0, tiled=True)  13.2 us
    all_gather x1, blocking collectives, sum_by_parts(): whole = lax.all_gather(own, axis).reshape(-1, *lines.shape[1:])  8.75 us
    all_to_all x1, starting transfers between devices, body(): lax.all_to_all(served, SA, split_axis=2, concat_axis=3, tiled=True)  7.19 us
    reduce_sum x5, other arithmetic, square_sums(): return jnp.sum(values * values, axis=dims_summed)  5.18 us
  transfers between devices with their start and end apart: 2, of which 1 were waited for; matrix products, arithmetic and copies ran while one was open for 1% of the time, Pallas kernels for 0%

commit v1 on v0

v1 whole, which is shorter than its diff:
```python
import functools

import jax
import jax.numpy as jnp
from jax import lax
from jax.experimental import pallas as pl
from jax.experimental.pallas import tpu as pltpu
from jax.sharding import PartitionSpec as P

MESH = pl.DeviceIdType.MESH
F32, BF16 = jnp.float32, jnp.bfloat16

SPAN = 2.0**7.875


def row_max(block8):
    return jnp.maximum(jnp.max(block8, axis=0, keepdims=True), 1e-30)


def round_up(scale):
    return (scale * 1.015625).astype(BF16)


def encoded(values, factor):
    u = values * factor
    u2 = u * u
    u4 = u2 * u2
    u8 = u4 * u4
    u16 = u8 * u8
    return jnp.where(u < 0, -u16, u16).astype(BF16)


def decoded(wire, factor):
    y = wire.astype(F32)
    root = lax.rsqrt(lax.rsqrt(lax.rsqrt(lax.rsqrt(jnp.abs(y)))))
    return jnp.where(y < 0, -root, root) * factor


def kernel(
    w1, w3, w2, gate,
    out_w1, out_w3, out_w2, out_gate, out_soup, out_rep,
    load, gload, sown, dsend, drecv, squares, rowsums,
    zsend, zrecv, gall, gdrecv, gshard, served, msgs, recv,
    load_sem, gload_sem, ds_sem, dr_sem, zs_sem, zr_sem, gd_sem, gz_sem, ga_sem, ms_sem, mr_sem,
):
    weights = (w1, w3, w2)
    row, sa = lax.axis_index("row"), lax.axis_index("sa")
    zh, core = row // 2, row % 2
    partner = row + 1 - 2 * core
    up, down = (row + 2) % 8, (row + 6) % 8

    chips = [(zh + d) % 4 for d in (2, 1, 3, 0)]

    def load_copy(k, t):
        return pltpu.make_async_copy(
            weights[t].at[:, pl.ds(2 * chips[k], 2)], load.at[k, t], load_sem.at[k, t]
        )

    gate_load = pltpu.make_async_copy(gate, gload, gload_sem)
    for t in range(3):
        load_copy(0, t).start()
    gate_load.start()

    barrier = pltpu.get_barrier_semaphore()
    for peer in (partner, up, down):
        pl.semaphore_signal(barrier, inc=1, device_id=(peer, sa), device_id_type=MESH)

    def greet(i, _):
        pl.semaphore_signal(barrier, inc=1, device_id=(row, (sa + i) % 32), device_id_type=MESH)
        return 0

    lax.fori_loop(1, 32, greet, 0)
    for k in range(1, 4):
        for t in range(3):
            load_copy(k, t).start()

    def chunk_sums(k, parity, dest):
        expert = 2 * chips[k] + parity
        top = jnp.zeros((8, 128), F32)
        for t in range(3):
            a, b = load[k, t, 0, parity], load[k, t, 1, parity]
            total = a + b
            dest[t * 128 : (t + 1) * 128, :] = total
            for r, v in ((0, a), (1, b)):
                index = pl.multiple_of((t * 16 + r * 8 + expert) * 8, 8)
                squares[pl.ds(index, 8), :] = jnp.sum((v * v).reshape(16, 8, 128), axis=0)
            if k < 3:
                top = jnp.maximum(top, jnp.max(jnp.abs(total).reshape(16, 8, 128), axis=0))
        if k < 3:
            dest[384:392, :] = top

    def d2d(k):
        return pltpu.make_async_remote_copy(
            src_ref=dsend.at[k], dst_ref=drecv.at[k], send_sem=ds_sem.at[k], recv_sem=dr_sem.at[k],
            device_id=(partner, sa), device_id_type=MESH,
        )

    def z_copy(way, stage, piece):
        rows = pl.ds(0, 80) if piece == 0 else pl.ds(16 + 64 * piece, 64)
        return pltpu.make_async_remote_copy(
            src_ref=zsend.at[way, stage, rows], dst_ref=zrecv.at[way, stage, rows],
            send_sem=zs_sem.at[way, stage, piece], recv_sem=zr_sem.at[way, stage, piece],
            device_id=((up, down)[way], sa), device_id_type=MESH,
        )

    def chip_rows(k, t, half):
        rows = slice(t * 128 + half * 64, t * 128 + half * 64 + 64)
        return sown[k, rows, :] + drecv[k, rows, :]

    def chip_top(k):
        return row_max(sown[k, 384:392, :] + drecv[k, 384:392, :])

    def put_scale(way, stage, scale):
        zsend[way, stage, 0:16, :] = jnp.broadcast_to(scale, (16, 128))
        return SPAN / scale.astype(F32)

    def z_piece(way, stage, t, values, factor):
        zsend[way, stage, 16 + 64 * t : 80 + 64 * t, :] = encoded(values, factor)
        z_copy(way, stage, t).start()

    def z_scale(way, stage):
        return zrecv[way, stage, 0:16, :].astype(F32)[0:1]

    def z_values(way, stage, t):
        return decoded(
            zrecv[way, stage, 16 + 64 * t : 80 + 64 * t, :], z_scale(way, stage) * (1 / SPAN)
        )

    def prepare(k):
        for t in range(3):
            load_copy(k, t).wait()
        chunk_sums(k, 1 - core, dsend.at[k])
        if k == 0:
            pl.semaphore_wait(barrier, 34)
        d2d(k).start()
        chunk_sums(k, core, sown.at[k])

    def gate_d2d():
        return pltpu.make_async_remote_copy(
            src_ref=gall.at[4], dst_ref=gdrecv, send_sem=gd_sem.at[0], recv_sem=gd_sem.at[1],
            device_id=(partner, sa), device_id_type=MESH,
        )

    def gate_copy(which):
        slot = (zh, zh, (zh + 3) % 4)[which]
        return pltpu.make_async_remote_copy(
            src_ref=gall.at[slot], dst_ref=gall.at[slot],
            send_sem=gz_sem.at[0, which], recv_sem=gz_sem.at[1, which],
            device_id=((up, down, up)[which], sa), device_id_type=MESH,
        )

    prepare(0)

    gate_load.wait()
    gall[4] = gload[0] + gload[1]
    gate_d2d().start()
    for r in range(2):
        rowsums[48 + 8 * r : 56 + 8 * r, :] = gload[r] * gload[r]

    prepare(1)

    d2d(0).wait_recv()
    scale = round_up(chip_top(0))
    factors = [put_scale(way, 0, scale) for way in range(2)]
    for t in range(3):
        for way in range(2):
            z_piece(way, 0, t, chip_rows(0, t, way), factors[way])

    gate_d2d().wait_recv()
    gall[zh] = gall[4] + gdrecv[...]
    gate_copy(0).start()
    gate_copy(1).start()

    prepare(2)

    tops = []
    for way in range(2):
        k = 1 + way
        d2d(k).wait_recv()
        tops.append(chip_top(k))
        factor = put_scale(way, 1, round_up(tops[way]))
        for t in range(3):
            z_piece(way, 1, t, chip_rows(k, t, 1 - way), factor)

    prepare(3)

    factors = []
    for t in range(3):
        for way in range(2):
            z_copy(way, 0, t).wait_recv()
            if t == 0:
                scale = round_up(tops[way] + z_scale(way, 0))
                factors.append(put_scale(way, 2, scale))
            values = chip_rows(1 + way, t, way) + z_values(way, 0, t)
            z_piece(way, 2, t, values, factors[way])

    gate_copy(0).wait_recv()
    gate_copy(2).start()
    gate_copy(1).wait_recv()
    gate_copy(2).wait_recv()
    gate_total = ((gall[0] + gall[1]) + gall[2]) + gall[3]
    gshard[...] = (gate_total * (1 / 16)).astype(BF16)

    def gate_send(i):
        return pltpu.make_async_remote_copy(
            src_ref=gshard, dst_ref=out_gate.at[:, pl.ds(pl.multiple_of(sa * 128, 128), 128)],
            send_sem=ga_sem.at[0], recv_sem=ga_sem.at[1],
            device_id=(row, (sa + i) % 32), device_id_type=MESH,
        )

    def gate_start(i, _):
        gate_send(i).start()
        return 0

    lax.fori_loop(1, 32, gate_start, 0)
    out_gate[:, pl.ds(pl.multiple_of(sa * 128, 128), 128)] = gshard[...]

    for t in range(3):
        part = squares[pl.ds(t * 128, 16, stride=8), :]
        for j in range(1, 8):
            part = part + squares[pl.ds(t * 128 + j, 16, stride=8), :]
        rowsums[16 * t : 16 * t + 16, :] = part
    rowsums[64:128, :] = jnp.zeros((64, 128), F32)
    norm_row = jnp.sum(rowsums[...].T, axis=0, keepdims=True)
    lane = lax.broadcasted_iota(jnp.int32, (1, 128), 1)

    d2d(3).wait_recv()
    for t in range(3):
        for half in range(2):
            total = chip_rows(3, t, half)
            z_copy(1 - half, 1, t).wait_recv()
            total = total + z_values(1 - half, 1, t)
            z_copy(half, 2, t).wait_recv()
            total = total + z_values(half, 2, t)
            served[t, 64 * half : 64 * half + 64, :] = (total * (1 / 16)).astype(BF16).astype(F32)
        final = served[t]
        square = jnp.sum(final * final, axis=(0, 1), keepdims=True)
        norm_row = jnp.where(lane == 64 + t, square, norm_row)

    high = norm_row.astype(BF16).astype(F32)
    rest = norm_row - high
    middle = rest.astype(BF16).astype(F32)
    tail = jnp.concatenate([high, middle, rest - middle, jnp.zeros((1, 128), F32)], axis=0)
    for p in range(32):
        parts = [served[t, 4 * p : 4 * p + 4, :] for t in range(3)]
        msgs[p] = jnp.concatenate(parts + [tail], axis=0).astype(BF16)

    def msg_send(i):
        return pltpu.make_async_remote_copy(
            src_ref=msgs.at[(sa + i) % 32], dst_ref=recv.at[sa],
            send_sem=ms_sem, recv_sem=mr_sem,
            device_id=(row, (sa + i) % 32), device_id_type=MESH,
        )

    def msg_start(i, _):
        msg_send(i).start()
        return 0

    lax.fori_loop(1, 32, msg_start, 0)
    recv[sa] = msgs[sa]

    for k in range(4):
        d2d(k).wait_send()
    for way in range(2):
        for stage in range(3):
            for t in range(3):
                z_copy(way, stage, t).wait_send()
    gate_d2d().wait_send()
    for which in range(3):
        gate_copy(which).wait_send()
    others = out_gate.at[:, pl.ds(0, 31 * 128)]
    pltpu.make_async_copy(others, others, ga_sem.at[0]).wait()
    pltpu.make_async_copy(others, others, ga_sem.at[1]).wait()

    gates = out_gate[...].astype(F32)
    mine = lax.broadcasted_iota(jnp.int32, gates.shape, 0) == row
    gate_square = jnp.sum(jnp.where(mine, gates * gates, 0.0), axis=(0, 1), keepdims=True)

    batch = recv.at[pl.ds(0, 31)]
    pltpu.make_async_copy(batch, batch, ms_sem).wait()
    pltpu.make_async_copy(batch, batch, mr_sem).wait()

    totals = jnp.zeros((4, 128), F32)
    for s in range(32):
        message = recv[s].astype(F32)
        for t, out in enumerate((out_w1, out_w3, out_w2)):
            out[0, :, 128 * s : 128 * s + 128] = message[4 * t : 4 * t + 4].astype(BF16)
        totals = totals + message[12:16]
    total_row = (totals[0:1] + totals[1:2]) + totals[2:3]

    wide = jnp.broadcast_to(total_row, (16, 128))
    lanes = lax.broadcasted_iota(jnp.int32, (16, 128), 1)
    rows = lax.broadcasted_iota(jnp.int32, (16, 128), 0)
    spread = jnp.zeros((16, 128), F32)
    for t in range(4):
        column = jnp.sum(jnp.where(lanes == rows + 16 * t, wide, 0.0), axis=1, keepdims=True)
        spread = jnp.where(lanes == t, column * (1 / (4096 if t == 3 else 524288)), spread)
    norms = jnp.sqrt(spread)
    for r in range(2):
        out_rep[r] = norms[8 * r : 8 * r + 8, 0:4]

    soup = jnp.where(lane == 3, gate_square * (1 / 4096), 0.0)
    for t in range(3):
        entry = jnp.sum(jnp.where(lane == 64 + t, total_row, 0.0), axis=1, keepdims=True)
        soup = jnp.where(lane == t, entry * (1 / 524288), soup)
    out_soup[...] = jnp.sqrt(soup)[:, 0:4]


def body(w1, w3, w2, gate):
    vmem = pl.BlockSpec(memory_space=pltpu.VMEM)
    hbm = pl.BlockSpec(memory_space=pl.ANY)
    dma = pltpu.SemaphoreType.DMA
    return pl.pallas_call(
        kernel,
        name="soup",
        out_shape=(
            jax.ShapeDtypeStruct((1, 4, 4096), BF16),
            jax.ShapeDtypeStruct((1, 4, 4096), BF16),
            jax.ShapeDtypeStruct((1, 4, 4096), BF16),
            jax.ShapeDtypeStruct((8, 4096), BF16),
            jax.ShapeDtypeStruct((1, 4), F32),
            jax.ShapeDtypeStruct((2, 8, 4), F32),
        ),
        in_specs=[hbm] * 4,
        out_specs=(vmem,) * 6,
        scratch_shapes=[
            pltpu.VMEM((4, 3, 2, 2, 128, 128), F32),
            pltpu.VMEM((2, 8, 128), F32),
            pltpu.VMEM((4, 392, 128), F32),
            pltpu.VMEM((4, 392, 128), F32),
            pltpu.VMEM((4, 392, 128), F32),
            pltpu.VMEM((384, 128), F32),
            pltpu.VMEM((128, 128), F32),
            pltpu.VMEM((2, 3, 208, 128), BF16),
            pltpu.VMEM((2, 3, 208, 128), BF16),
            pltpu.VMEM((5, 8, 128), F32),
            pltpu.VMEM((8, 128), F32),
            pltpu.VMEM((8, 128), BF16),
            pltpu.VMEM((3, 128, 128), F32),
            pltpu.VMEM((32, 16, 128), BF16),
            pltpu.VMEM((32, 16, 128), BF16),
            dma((4, 3)),
            dma,
            dma((4,)),
            dma((4,)),
            dma((2, 3, 3)),
            dma((2, 3, 3)),
            dma((2,)),
            dma((2, 3)),
            dma((2,)),
            dma,
            dma,
        ],
        compiler_params=pltpu.CompilerParams(collective_id=0, has_side_effects=True),
    )(w1, w3, w2, gate)


def solution(mesh):
    in_specs = (
        P("row", None, None, "sa"),
        P("row", None, None, "sa"),
        P("row", None, None, "sa"),
        P("row", None, "sa"),
    )
    out_specs = (
        P("row", "sa", None),
        P("row", "sa", None),
        P("row", "sa", None),
        P(),
        P("row", None),
        P("row", None, None),
    )
    return jax.shard_map(body, mesh=mesh, in_specs=in_specs, out_specs=out_specs, check_vma=False)
```

time: 132 us -> 34.9 us (0.26)
  blocking collectives: 81.3 us -> 0 us
  Pallas kernels: 0 us -> 28.6 us
  between operations: 14.1 us -> 0.66 us
  waiting for transfers between devices: 13.2 us -> 0 us
  other arithmetic: 9.41 us -> 0 us
  starting transfers between devices: 7.23 us -> 0 us
    all_gather x4 -> x0, blocking collectives: 37 us -> none  [the longest x3 28.3 us: stacked_from(): blocks = lax.all_gather(blocks, axes[k])]
    pallas_call x0 -> x1, Pallas kernels: none -> 28.6 us  [body(): pl.pallas_call(kernel, name='soup', out_shape=(jax.ShapeDtypeStruct((1, 4...]
    psum x3 -> x0, blocking collectives: 23.8 us -> none  [by_axis(): return functools.reduce(lax.psum, axes, array)]
    unnamed x1 -> x0, blocking collectives: 20.5 us -> none
    reduce_scatter x1 -> x0, waiting for transfers between devices: 13.2 us -> none  [own_rows_2(): own = lax.psum_scatter(everything, axis, scatter_dimension=0, tiled=True)]
    all_to_all x1 -> x0, starting transfers between devices: 7.19 us -> none  [body(): lax.all_to_all(served, SA, split_axis=2, concat_axis=3, tiled=True)]
    reduce_sum x5 -> x0, other arithmetic: 5.18 us -> none  [square_sums(): return jnp.sum(values * values, axis=dims_summed)]
    another operation x3 -> x0, other arithmetic: 2.68 us -> none  [the longest x1 2.57 us: body(): jnp.stack([square_sums(served.astype(jnp.float32), (1, 2)) for served in...]
  transfers between devices with their start and end apart: 2 -> 0, of which waited for: 1 -> 0; matrix products, arithmetic and copies ran while one was open for 1% -> 0% of each run, Pallas kernels for 0% -> 0%
where the time goes in v1:
time: 34.9 us; the launch traced here: 34.4 us
  Pallas kernels  28.6 us (82%)
  local copies, waits for them, and re-layouts  5.14 us (15%)
  between operations  0.66 us (2%)
    pallas_call x1, Pallas kernels, body(): pl.pallas_call(kernel, name='soup', out_shape=(jax.ShapeDtypeStruct((1, 4...  28.6 us
    unnamed x15, local copies, waits for them, and re-layouts  4.46 us

profile of v1, /device:TPU:2, one launch (start us, length us, event | category | flops | bytes accessed | tf_op | source)
XLA Modules:
  0.0 34.4 jit_solution(13861630995797826134)
XLA Ops:
  0.6 28.6 %soup.1 = (bf16[1,4,4096]{2,1,0:T(4,128)(2,1)}, bf16[1,4,4096]{2,1,0:T(4,128)(2,1)}, bf16[1,4,4096]{2,1,0:T(4,128)(2,1)}, bf16[8,4096]{1,0:T(8,128)(2,1)}, f32[1,4]{1,0:T(1,128)}, /*index=5*/f32[2,8,4]{2,1,0:T(8,128)}) custom-call(f32[2,8,128,128]{3,2,1,0:T(8,128)} %w1.1, f32[2,8,128,128]{3,2,1,0:T(8,128)} %w3.1, f32[2,8,128,128]{3,2,1,0:T(8,128)} %w2.1, ...), custom_call_target="tpu_custom_call" | custom-call | tf_op jit(solution)/shard_map/soup/pallas_call | solution.py:313
  29.2 0.0 copy-start.3
  29.2 0.7 %copy-done.3 = f32[2,8,4]{2,1,0:T(8,128)S(1)} copy-done((f32[2,8,4]{2,1,0:T(8,128)S(1)}, f32[2,8,4]{2,1,0:T(8,128)}, u32[]{:S(2)}) %copy-start.3) | copy-done | bytes 280
  29.9 0.7 %copy.10 = f32[2,8,4]{1,2,0:T(4,128)} copy(f32[2,8,4]{2,1,0:T(8,128)S(1)} %copy-done.3) | data formatting | bytes 512 | tf_op jit(solution)/shard_map/soup/pallas_call | solution.py:313
  30.6 0.0 copy-start.2
  30.6 0.0 copy-start.1
  30.6 1.4 %copy.16 = bf16[1,4,4096]{2,1,0:T(4,128)(2,1)} copy(bf16[1,4,4096]{2,1,0:T(4,128)(2,1)} %get-tuple-element.18) | data formatting | bytes 65536
  32.0 0.0 copy-done.2
  32.0 0.0 copy-start
  32.0 0.6 %copy.17 = bf16[1,4,4096]{2,1,0:T(4,128)(2,1)} copy(bf16[1,4,4096]{2,1,0:T(4,128)(2,1)S(1)} %copy-done.2) | data formatting | bytes 65536
  32.6 0.0 copy-done.1
  32.6 0.6 %copy.18 = bf16[1,4,4096]{2,1,0:T(4,128)(2,1)} copy(bf16[1,4,4096]{2,1,0:T(4,128)(2,1)S(1)} %copy-done.1) | data formatting | bytes 65536
  33.2 0.0 copy-done
  33.2 0.0 copy-start.4
  33.2 0.6 %copy.19 = bf16[8,4096]{1,0:T(8,128)(2,1)} copy(bf16[8,4096]{1,0:T(8,128)(2,1)S(1)} %copy-done) | data formatting | bytes 131072
  33.9 0.0 copy-done.4
  33.9 0.5 %copy.20 = f32[1,4]{1,0:T(1,128)} copy(f32[1,4]{1,0:T(1,128)S(1)} %copy-done.4) | data formatting | bytes 32
Async XLA Ops:
  29.2 0.7 %copy-start.3 = (f32[2,8,4]{2,1,0:T(8,128)S(1)}, f32[2,8,4]{2,1,0:T(8,128)}, u32[]{:S(2)}) copy-start(f32[2,8,4]{2,1,0:T(8,128)} %get-tuple-element.11) | copy-start | bytes 772
  30.6 1.4 %copy-start.2 = (bf16[1,4,4096]{2,1,0:T(4,128)(2,1)S(1)}, bf16[1,4,4096]{2,1,0:T(4,128)(2,1)}, u32[]{:S(2)}) copy-start(bf16[1,4,4096]{2,1,0:T(4,128)(2,1)} %get-tuple-element.19) | copy-start | bytes 98308
  30.6 2.0 %copy-start.1 = (bf16[1,4,4096]{2,1,0:T(4,128)(2,1)S(1)}, bf16[1,4,4096]{2,1,0:T(4,128)(2,1)}, u32[]{:S(2)}) copy-start(bf16[1,4,4096]{2,1,0:T(4,128)(2,1)} %get-tuple-element.20) | copy-start | bytes 98308
  32.0 1.2 %copy-start = (bf16[8,4096]{1,0:T(8,128)(2,1)S(1)}, bf16[8,4096]{1,0:T(8,128)(2,1)}, u32[]{:S(2)}) copy-start(bf16[8,4096]{1,0:T(8,128)(2,1)} %get-tuple-element.21) | copy-start | bytes 196612
  33.2 0.6 %copy-start.4 = (f32[1,4]{1,0:T(1,128)S(1)}, f32[1,4]{1,0:T(1,128)}, u32[]{:S(2)}) copy-start(f32[1,4]{1,0:T(1,128)} %get-tuple-element.22) | copy-start | bytes 52

commit v2 on v1

--- a/solution.py
+++ b/solution.py
@@ -38,10 +38,10 @@
 
 def kernel(
     w1, w3, w2, gate,
-    out_w1, out_w3, out_w2, out_gate, out_soup, out_rep,
+    recv, out_gate,
     load, gload, sown, dsend, drecv, squares, rowsums,
-    zsend, zrecv, gall, gdrecv, gshard, served, msgs, recv,
-    load_sem, gload_sem, ds_sem, dr_sem, zs_sem, zr_sem, gd_sem, gz_sem, ga_sem, ms_sem, mr_sem,
+    zsend, zrecv, gall, gdrecv, gshard, served, msgs,
+    load_sem, gload_sem, ds_sem, dr_sem, zs_sem, zr_sem, gd_sem, gz_sem, ga_sem, ms_sem, mr_sem, known,
 ):
     weights = (w1, w3, w2)
     row, sa = lax.axis_index("row"), lax.axis_index("sa")
@@ -57,19 +57,17 @@
         )
 
     gate_load = pltpu.make_async_copy(gate, gload, gload_sem)
+    gate_load.start()
     for t in range(3):
         load_copy(0, t).start()
-    gate_load.start()
-
+
+    zl, x, y = sa // 16, (sa // 4) % 4, sa % 4
+    x_line = [(row, zl * 16 + ((x + i) % 4) * 4 + y) for i in (1, 2, 3)]
+    y_line = [(row, zl * 16 + x * 4 + (y + i) % 4) for i in (1, 2, 3)]
+    z_pair = (row, sa + 16 - 32 * zl)
     barrier = pltpu.get_barrier_semaphore()
-    for peer in (partner, up, down):
-        pl.semaphore_signal(barrier, inc=1, device_id=(peer, sa), device_id_type=MESH)
-
-    def greet(i, _):
-        pl.semaphore_signal(barrier, inc=1, device_id=(row, (sa + i) % 32), device_id_type=MESH)
-        return 0
-
-    lax.fori_loop(1, 32, greet, 0)
+    for device in [(up, sa), (down, sa), (partner, sa), *x_line, *y_line, z_pair]:
+        pl.semaphore_signal(barrier, inc=1, device_id=device, device_id_type=MESH)
     for k in range(1, 4):
         for t in range(3):
             load_copy(k, t).start()
@@ -131,8 +129,12 @@
             load_copy(k, t).wait()
         chunk_sums(k, 1 - core, dsend.at[k])
         if k == 0:
-            pl.semaphore_wait(barrier, 34)
+            pl.semaphore_wait(barrier, 10)
+            gate_d2d().start()
         d2d(k).start()
+        if k == 0:
+            for device in x_line:
+                pl.semaphore_signal(known.at[0], inc=1, device_id=device, device_id_type=MESH)
         chunk_sums(k, core, sown.at[k])
 
     def gate_d2d():
@@ -149,29 +151,29 @@
             device_id=((up, down, up)[which], sa), device_id_type=MESH,
         )
 
-    prepare(0)
-
     gate_load.wait()
     gall[4] = gload[0] + gload[1]
-    gate_d2d().start()
     for r in range(2):
         rowsums[48 + 8 * r : 56 + 8 * r, :] = gload[r] * gload[r]
 
+    prepare(0)
     prepare(1)
-
-    d2d(0).wait_recv()
-    scale = round_up(chip_top(0))
-    factors = [put_scale(way, 0, scale) for way in range(2)]
-    for t in range(3):
-        for way in range(2):
-            z_piece(way, 0, t, chip_rows(0, t, way), factors[way])
 
     gate_d2d().wait_recv()
     gall[zh] = gall[4] + gdrecv[...]
     gate_copy(0).start()
     gate_copy(1).start()
 
+    d2d(0).wait_recv()
+    scale = round_up(chip_top(0))
+    factors = [put_scale(way, 0, scale) for way in range(2)]
+    for t in range(3):
+        for way in range(2):
+            z_piece(way, 0, t, chip_rows(0, t, way), factors[way])
+
     prepare(2)
+    pl.semaphore_wait(known.at[0], 3)
+    pl.semaphore_signal(known.at[1], inc=1, device_id=z_pair, device_id_type=MESH)
 
     tops = []
     for way in range(2):
@@ -183,6 +185,8 @@
             z_piece(way, 1, t, chip_rows(k, t, 1 - way), factor)
 
     prepare(3)
+    gate_copy(0).wait_recv()
+    gate_copy(2).start()
 
     factors = []
     for t in range(3):
@@ -194,8 +198,6 @@
             values = chip_rows(1 + way, t, way) + z_values(way, 0, t)
             z_piece(way, 2, t, values, factors[way])
 
-    gate_copy(0).wait_recv()
-    gate_copy(2).start()
     gate_copy(1).wait_recv()
     gate_copy(2).wait_recv()
     gate_total = ((gall[0] + gall[1]) + gall[2]) + gall[3]
@@ -212,6 +214,7 @@
         gate_send(i).start()
         return 0
 
+    pl.semaphore_wait(known.at[1], 1)
     lax.fori_loop(1, 32, gate_start, 0)
     out_gate[:, pl.ds(pl.multiple_of(sa * 128, 128), 128)] = gshard[...]
 
@@ -223,6 +226,21 @@
     rowsums[64:128, :] = jnp.zeros((64, 128), F32)
     norm_row = jnp.sum(rowsums[...].T, axis=0, keepdims=True)
     lane = lax.broadcasted_iota(jnp.int32, (1, 128), 1)
+
+    def msg_send(piece, i):
+        return pltpu.make_async_remote_copy(
+            src_ref=msgs.at[piece, (sa + i) % 32], dst_ref=recv.at[piece, sa],
+            send_sem=ms_sem.at[piece], recv_sem=mr_sem.at[piece],
+            device_id=(row, (sa + i) % 32), device_id_type=MESH,
+        )
+
+    def send_all(piece):
+        def start(i, _):
+            msg_send(piece, i).start()
+            return 0
+
+        lax.fori_loop(1, 32, start, 0)
+        recv[piece, sa] = msgs[piece, sa]
 
     d2d(3).wait_recv()
     for t in range(3):
@@ -236,28 +254,19 @@
         final = served[t]
         square = jnp.sum(final * final, axis=(0, 1), keepdims=True)
         norm_row = jnp.where(lane == 64 + t, square, norm_row)
+        if t == 1:
+            for p in range(32):
+                parts = [served[j, 4 * p : 4 * p + 4, :] for j in range(2)]
+                msgs[0, p] = jnp.concatenate(parts, axis=0).astype(BF16)
+            send_all(0)
 
     high = norm_row.astype(BF16).astype(F32)
     rest = norm_row - high
     middle = rest.astype(BF16).astype(F32)
     tail = jnp.concatenate([high, middle, rest - middle, jnp.zeros((1, 128), F32)], axis=0)
     for p in range(32):
-        parts = [served[t, 4 * p : 4 * p + 4, :] for t in range(3)]
-        msgs[p] = jnp.concatenate(parts + [tail], axis=0).astype(BF16)
-
-    def msg_send(i):
-        return pltpu.make_async_remote_copy(
-            src_ref=msgs.at[(sa + i) % 32], dst_ref=recv.at[sa],
-            send_sem=ms_sem, recv_sem=mr_sem,
-            device_id=(row, (sa + i) % 32), device_id_type=MESH,
-        )
-
-    def msg_start(i, _):
-        msg_send(i).start()
-        return 0
-
-    lax.fori_loop(1, 32, msg_start, 0)
-    recv[sa] = msgs[sa]
+        msgs[1, p] = jnp.concatenate([served[2, 4 * p : 4 * p + 4, :], tail], axis=0).astype(BF16)
+    send_all(1)
 
     for k in range(4):
         d2d(k).wait_send()
@@ -272,57 +281,55 @@
     pltpu.make_async_copy(others, others, ga_sem.at[0]).wait()
     pltpu.make_async_copy(others, others, ga_sem.at[1]).wait()
 
-    gates = out_gate[...].astype(F32)
-    mine = lax.broadcasted_iota(jnp.int32, gates.shape, 0) == row
-    gate_square = jnp.sum(jnp.where(mine, gates * gates, 0.0), axis=(0, 1), keepdims=True)
-
-    batch = recv.at[pl.ds(0, 31)]
-    pltpu.make_async_copy(batch, batch, ms_sem).wait()
-    pltpu.make_async_copy(batch, batch, mr_sem).wait()
+    for piece in range(2):
+        batch = recv.at[piece, pl.ds(0, 31)]
+        pltpu.make_async_copy(batch, batch, ms_sem.at[piece]).wait()
+        pltpu.make_async_copy(batch, batch, mr_sem.at[piece]).wait()
+
+
+def unpack(recv, gates, out_w1, out_w3, out_w2, out_gate, out_soup, out_rep):
+    row = lax.axis_index("row")
+    routed = gates[...]
+    out_gate[...] = routed
+    wide = routed.astype(F32)
+    mine = lax.broadcasted_iota(jnp.int32, wide.shape, 0) == row
+    gate_square = jnp.sum(jnp.where(mine, wide * wide, 0.0), axis=(0, 1), keepdims=True)
 
     totals = jnp.zeros((4, 128), F32)
     for s in range(32):
-        message = recv[s].astype(F32)
-        for t, out in enumerate((out_w1, out_w3, out_w2)):
-            out[0, :, 128 * s : 128 * s + 128] = message[4 * t : 4 * t + 4].astype(BF16)
-        totals = totals + message[12:16]
+        columns = slice(128 * s, 128 * s + 128)
+        first = recv[0, s].astype(F32)
+        last = recv[1, s].astype(F32)
+        out_w1[0, :, columns] = first[0:4].astype(BF16)
+        out_w3[0, :, columns] = first[4:8].astype(BF16)
+        out_w2[0, :, columns] = last[0:4].astype(BF16)
+        totals = totals + last[4:8]
     total_row = (totals[0:1] + totals[1:2]) + totals[2:3]
 
-    wide = jnp.broadcast_to(total_row, (16, 128))
-    lanes = lax.broadcasted_iota(jnp.int32, (16, 128), 1)
-    rows = lax.broadcasted_iota(jnp.int32, (16, 128), 0)
-    spread = jnp.zeros((16, 128), F32)
-    for t in range(4):
-        column = jnp.sum(jnp.where(lanes == rows + 16 * t, wide, 0.0), axis=1, keepdims=True)
-        spread = jnp.where(lanes == t, column * (1 / (4096 if t == 3 else 524288)), spread)
-    norms = jnp.sqrt(spread)
+    lane = lax.broadcasted_iota(jnp.int32, (1, 128), 1)
     for r in range(2):
-        out_rep[r] = norms[8 * r : 8 * r + 8, 0:4]
-
-    soup = jnp.where(lane == 3, gate_square * (1 / 4096), 0.0)
-    for t in range(3):
-        entry = jnp.sum(jnp.where(lane == 64 + t, total_row, 0.0), axis=1, keepdims=True)
-        soup = jnp.where(lane == t, entry * (1 / 524288), soup)
-    out_soup[...] = jnp.sqrt(soup)[:, 0:4]
+        for t in range(4):
+            entries = pltpu.roll(total_row, 128 - (16 * t + 8 * r) if t + r else 0, 1)
+            norms = jnp.sqrt(entries * (1 / (4096 if t == 3 else 524288)))
+            out_rep[r, t : t + 1, :] = norms[:, 0:8]
+    soup = pltpu.roll(total_row, 64, 1) * (1 / 524288)
+    soup = jnp.sqrt(jnp.where(lane == 3, gate_square * (1 / 4096), soup))
+    out_soup[...] = soup[:, 0:4]
 
 
 def body(w1, w3, w2, gate):
     vmem = pl.BlockSpec(memory_space=pltpu.VMEM)
     hbm = pl.BlockSpec(memory_space=pl.ANY)
     dma = pltpu.SemaphoreType.DMA
-    return pl.pallas_call(
+    recv, gates = pl.pallas_call(
         kernel,
         name="soup",
         out_shape=(
-            jax.ShapeDtypeStruct((1, 4, 4096), BF16),
-            jax.ShapeDtypeStruct((1, 4, 4096), BF16),
-            jax.ShapeDtypeStruct((1, 4, 4096), BF16),
+            jax.ShapeDtypeStruct((2, 32, 8, 128), BF16),
             jax.ShapeDtypeStruct((8, 4096), BF16),
-            jax.ShapeDtypeStruct((1, 4), F32),
-            jax.ShapeDtypeStruct((2, 8, 4), F32),
         ),
         in_specs=[hbm] * 4,
-        out_specs=(vmem,) * 6,
+        out_specs=(vmem,) * 2,
         scratch_shapes=[
             pltpu.VMEM((4, 3, 2, 2, 128, 128), F32),
             pltpu.VMEM((2, 8, 128), F32),
@@ -337,8 +344,7 @@
             pltpu.VMEM((8, 128), F32),
             pltpu.VMEM((8, 128), BF16),
             pltpu.VMEM((3, 128, 128), F32),
-            pltpu.VMEM((32, 16, 128), BF16),
-            pltpu.VMEM((32, 16, 128), BF16),
+            pltpu.VMEM((2, 32, 8, 128), BF16),
             dma((4, 3)),
             dma,
             dma((4,)),
@@ -348,11 +354,27 @@
             dma((2,)),
             dma((2, 3)),
             dma((2,)),
-            dma,
-            dma,
+            dma((2,)),
+            dma((2,)),
+            pltpu.SemaphoreType.REGULAR((2,)),
         ],
         compiler_params=pltpu.CompilerParams(collective_id=0, has_side_effects=True),
     )(w1, w3, w2, gate)
+    outs = pl.pallas_call(
+        unpack,
+        name="unpack",
+        out_shape=(
+            jax.ShapeDtypeStruct((1, 4, 4096), BF16),
+            jax.ShapeDtypeStruct((1, 4, 4096), BF16),
+            jax.ShapeDtypeStruct((1, 4, 4096), BF16),
+            jax.ShapeDtypeStruct((8, 4096), BF16),
+            jax.ShapeDtypeStruct((1, 4), F32),
+            jax.ShapeDtypeStruct((2, 4, 8), F32),
+        ),
+        in_specs=[vmem] * 2,
+        out_specs=(vmem,) * 6,
+    )(recv, gates)
+    return (*outs[:5], outs[5].transpose(0, 2, 1))
 
 
 def solution(mesh):

time: 34.9 us -> 29.4 us (0.84)
  the two profiles are of different devices: /device:TPU:2 before, /device:TPU:1 now
where the time goes in v2:
time: 29.4 us; the launch traced here: 29.3 us
  Pallas kernels  28.7 us (98%)
  between operations  0.64 us (2%)
    pallas_call x1, Pallas kernels, body(): pl.pallas_call(kernel, name='soup', out_shape=(jax.ShapeDtypeStruct((2, 3...  27.1 us
    pallas_call x1, Pallas kernels, body(): pl.pallas_call(unpack, name='unpack', out_shape=(jax.ShapeDtypeStruct((1,...  1.64 us

profile of v2, /device:TPU:1, one launch (start us, length us, event | category | flops | bytes accessed | tf_op | source)
XLA Modules:
  0.0 29.3 jit_solution(15814708091132765997)
XLA Ops:
  0.6 27.1 %soup.1 = (bf16[2,32,8,128]{3,2,1,0:T(8,128)(2,1)}, bf16[8,4096]{1,0:T(8,128)(2,1)}) custom-call(f32[2,8,128,128]{3,2,1,0:T(8,128)} %w1.1, f32[2,8,128,128]{3,2,1,0:T(8,128)} %w3.1, f32[2,8,128,128]{3,2,1,0:T(8,128)} %w2.1, f32[2,8,128]{2,1,0:T(8,128)} %gate.1), custom_call_target="tpu_custom_call" | custom-call | tf_op jit(solution)/shard_map/soup/pallas_call | solution.py:324
  27.7 1.6 %unpack.1 = (bf16[1,4,4096]{2,1,0:T(4,128)(2,1)}, bf16[1,4,4096]{2,1,0:T(4,128)(2,1)}, bf16[1,4,4096]{2,1,0:T(4,128)(2,1)}, bf16[8,4096]{1,0:T(8,128)(2,1)}, f32[1,4]{1,0:T(1,128)}, /*index=5*/f32[2,4,8]{2,1,0:T(4,128)}) custom-call(bf16[2,32,8,128]{3,2,1,0:T(8,128)(2,1)} %get-tuple-element.14.recv, bf16[8,4096]{1,0:T(8,128)(2,1)} %get-tuple-element.15.gates), custom_call_target="tpu_custom_call" | custom-call | tf_op jit(solution)/shard_map/unpack/pallas_call | solution.py:363

commit v3 on v2

--- a/solution.py
+++ b/solution.py
@@ -325,8 +325,8 @@
         kernel,
         name="soup",
         out_shape=(
-            jax.ShapeDtypeStruct((2, 32, 8, 128), BF16),
-            jax.ShapeDtypeStruct((8, 4096), BF16),
+            pltpu.VMEM((2, 32, 8, 128), BF16),
+            pltpu.VMEM((8, 4096), BF16),
         ),
         in_specs=[hbm] * 4,
         out_specs=(vmem,) * 2,
@@ -358,7 +358,7 @@
             dma((2,)),
             pltpu.SemaphoreType.REGULAR((2,)),
         ],
-        compiler_params=pltpu.CompilerParams(collective_id=0, has_side_effects=True),
+        compiler_params=pltpu.CompilerParams(collective_id=0, has_side_effects=True, vmem_limit_bytes=56 * 2**20),
     )(w1, w3, w2, gate)
     outs = pl.pallas_call(
         unpack,
@@ -373,6 +373,7 @@
         ),
         in_specs=[vmem] * 2,
         out_specs=(vmem,) * 6,
+        compiler_params=pltpu.CompilerParams(vmem_limit_bytes=4 * 2**20),
     )(recv, gates)
     return (*outs[:5], outs[5].transpose(0, 2, 1))
 

time: 29.4 us -> 27.8 us (0.946)
  Pallas kernels: 28.7 us -> 27.1 us
    pallas_call x1, Pallas kernels: 1.64 us -> 0.73 us  [body(): pl.pallas_call(unpack, name='unpack', out_shape=(jax.ShapeDtypeStruct((1,...]
    pallas_call x1, Pallas kernels: 27.1 us -> 26.4 us  [body(): pl.pallas_call(kernel, name='soup', out_shape=(pltpu.VMEM((2, 32, 8, 128)...]
where the time goes in v3:
time: 27.8 us
  Pallas kernels  27.1 us (97%)
  between operations  0.64 us (2%)
    pallas_call x1, Pallas kernels, body(): pl.pallas_call(kernel, name='soup', out_shape=(pltpu.VMEM((2, 32, 8, 128)...  26.4 us
    pallas_call x1, Pallas kernels, body(): pl.pallas_call(unpack, name='unpack', out_shape=(jax.ShapeDtypeStruct((1,...  0.73 us

profile of v3, /device:TPU:1, one launch (start us, length us, event | category | flops | bytes accessed | tf_op | source)
XLA Modules:
  0.0 27.8 jit_solution(4200329624157932901)
XLA Ops:
  0.6 26.4 %soup.1 = (bf16[2,32,8,128]{3,2,1,0:T(8,128)(2,1)S(1)}, bf16[8,4096]{1,0:T(8,128)(2,1)S(1)}) custom-call(f32[2,8,128,128]{3,2,1,0:T(8,128)} %w1.1, f32[2,8,128,128]{3,2,1,0:T(8,128)} %w3.1, f32[2,8,128,128]{3,2,1,0:T(8,128)} %w2.1, f32[2,8,128]{2,1,0:T(8,128)} %gate.1), custom_call_target="tpu_custom_call" | custom-call | tf_op jit(solution)/shard_map/soup/pallas_call | solution.py:324
  27.0 0.7 %unpack.1 = (bf16[1,4,4096]{2,1,0:T(4,128)(2,1)}, bf16[1,4,4096]{2,1,0:T(4,128)(2,1)}, bf16[1,4,4096]{2,1,0:T(4,128)(2,1)}, bf16[8,4096]{1,0:T(8,128)(2,1)}, f32[1,4]{1,0:T(1,128)}, /*index=5*/f32[2,4,8]{2,1,0:T(4,128)}) custom-call(bf16[2,32,8,128]{3,2,1,0:T(8,128)(2,1)S(1)} %get-tuple-element.14.recv, bf16[8,4096]{1,0:T(8,128)(2,1)S(1)} %get-tuple-element.15.gates), custom_call_target="tpu_custom_call" | custom-call | tf_op jit(solution)/shard_map/unpack/pallas_call | solution.py:363

commit v4 on v3

--- a/solution.py
+++ b/solution.py
@@ -11,6 +11,13 @@
 F32, BF16 = jnp.float32, jnp.bfloat16
 
 SPAN = 2.0**7.875
+
+
+STEPS = sorted(
+    [(dz, dx, dy) for dz in (0, 1) for dx in range(4) for dy in range(4) if dz + dx + dy],
+    key=lambda d: -(d[0] + min(d[1], 4 - d[1]) + min(d[2], 4 - d[2])),
+)
+FIRST, BLOCK = 8, 32
 
 
 def row_max(block8):
@@ -62,9 +69,11 @@
         load_copy(0, t).start()
 
     zl, x, y = sa // 16, (sa // 4) % 4, sa % 4
-    x_line = [(row, zl * 16 + ((x + i) % 4) * 4 + y) for i in (1, 2, 3)]
-    y_line = [(row, zl * 16 + x * 4 + (y + i) % 4) for i in (1, 2, 3)]
-    z_pair = (row, sa + 16 - 32 * zl)
+    zs, xs, ys = [zl * 16, 16 - zl * 16], [((x + i) % 4) * 4 for i in range(4)], [(y + i) % 4 for i in range(4)]
+    x_line = [(row, zs[0] + xs[i] + y) for i in (1, 2, 3)]
+    y_line = [(row, zs[0] + xs[0] + ys[i]) for i in (1, 2, 3)]
+    z_pair = (row, zs[1] + xs[0] + y)
+    sa_peers = [zs[dz] + xs[dx] + ys[dy] for dz, dx, dy in STEPS]
     barrier = pltpu.get_barrier_semaphore()
     for device in [(up, sa), (down, sa), (partner, sa), *x_line, *y_line, z_pair]:
         pl.semaphore_signal(barrier, inc=1, device_id=device, device_id_type=MESH)
@@ -94,35 +103,38 @@
         )
 
     def z_copy(way, stage, piece):
-        rows = pl.ds(0, 80) if piece == 0 else pl.ds(16 + 64 * piece, 64)
+        if stage == 1:
+            rows = pl.ds(0, FIRST + 192)
+        elif piece == 0:
+            rows = pl.ds(0, FIRST + BLOCK)
+        else:
+            rows = pl.ds(FIRST + BLOCK * piece, BLOCK)
         return pltpu.make_async_remote_copy(
             src_ref=zsend.at[way, stage, rows], dst_ref=zrecv.at[way, stage, rows],
             send_sem=zs_sem.at[way, stage, piece], recv_sem=zr_sem.at[way, stage, piece],
             device_id=((up, down)[way], sa), device_id_type=MESH,
         )
 
-    def chip_rows(k, t, half):
-        rows = slice(t * 128 + half * 64, t * 128 + half * 64 + 64)
-        return sown[k, rows, :] + drecv[k, rows, :]
+    def chip_rows(k, piece, half):
+        t, part = piece // 2, piece % 2
+        start = t * 128 + half * 64 + part * BLOCK
+        return sown[k, start : start + BLOCK, :] + drecv[k, start : start + BLOCK, :]
 
     def chip_top(k):
         return row_max(sown[k, 384:392, :] + drecv[k, 384:392, :])
 
     def put_scale(way, stage, scale):
-        zsend[way, stage, 0:16, :] = jnp.broadcast_to(scale, (16, 128))
+        zsend[way, stage, 0:FIRST, :] = jnp.broadcast_to(scale, (FIRST, 128))
         return SPAN / scale.astype(F32)
 
-    def z_piece(way, stage, t, values, factor):
-        zsend[way, stage, 16 + 64 * t : 80 + 64 * t, :] = encoded(values, factor)
-        z_copy(way, stage, t).start()
+    def block(piece):
+        return slice(FIRST + BLOCK * piece, FIRST + BLOCK * piece + BLOCK)
 
     def z_scale(way, stage):
-        return zrecv[way, stage, 0:16, :].astype(F32)[0:1]
-
-    def z_values(way, stage, t):
-        return decoded(
-            zrecv[way, stage, 16 + 64 * t : 80 + 64 * t, :], z_scale(way, stage) * (1 / SPAN)
-        )
+        return zrecv[way, stage, 0:FIRST, :].astype(F32)[0:1]
+
+    def z_values(way, stage, piece):
+        return decoded(zrecv[way, stage, block(piece), :], z_scale(way, stage) * (1 / SPAN))
 
     def prepare(k):
         for t in range(3):
@@ -133,6 +145,7 @@
             gate_d2d().start()
         d2d(k).start()
         if k == 0:
+            pl.semaphore_signal(known.at[2], inc=1, device_id=(up, sa), device_id_type=MESH)
             for device in x_line:
                 pl.semaphore_signal(known.at[0], inc=1, device_id=device, device_id_type=MESH)
         chunk_sums(k, core, sown.at[k])
@@ -144,11 +157,10 @@
         )
 
     def gate_copy(which):
-        slot = (zh, zh, (zh + 3) % 4)[which]
         return pltpu.make_async_remote_copy(
-            src_ref=gall.at[slot], dst_ref=gall.at[slot],
+            src_ref=gall.at[zh], dst_ref=gall.at[zh],
             send_sem=gz_sem.at[0, which], recv_sem=gz_sem.at[1, which],
-            device_id=((up, down, up)[which], sa), device_id_type=MESH,
+            device_id=((up, down, (row + 4) % 8)[which], sa), device_id_type=MESH,
         )
 
     gate_load.wait()
@@ -161,15 +173,17 @@
 
     gate_d2d().wait_recv()
     gall[zh] = gall[4] + gdrecv[...]
-    gate_copy(0).start()
-    gate_copy(1).start()
+    pl.semaphore_wait(known.at[2], 1)
+    for which in (2, 0, 1):
+        gate_copy(which).start()
 
     d2d(0).wait_recv()
     scale = round_up(chip_top(0))
     factors = [put_scale(way, 0, scale) for way in range(2)]
-    for t in range(3):
+    for piece in range(6):
         for way in range(2):
-            z_piece(way, 0, t, chip_rows(0, t, way), factors[way])
+            zsend[way, 0, block(piece), :] = encoded(chip_rows(0, piece, way), factors[way])
+            z_copy(way, 0, piece).start()
 
     prepare(2)
     pl.semaphore_wait(known.at[0], 3)
@@ -181,41 +195,35 @@
         d2d(k).wait_recv()
         tops.append(chip_top(k))
         factor = put_scale(way, 1, round_up(tops[way]))
-        for t in range(3):
-            z_piece(way, 1, t, chip_rows(k, t, 1 - way), factor)
+        for piece in range(6):
+            zsend[way, 1, block(piece), :] = encoded(chip_rows(k, piece, 1 - way), factor)
+        z_copy(way, 1, 0).start()
 
     prepare(3)
-    gate_copy(0).wait_recv()
-    gate_copy(2).start()
 
     factors = []
-    for t in range(3):
+    for piece in range(6):
         for way in range(2):
-            z_copy(way, 0, t).wait_recv()
-            if t == 0:
+            z_copy(way, 0, piece).wait_recv()
+            if piece == 0:
                 scale = round_up(tops[way] + z_scale(way, 0))
                 factors.append(put_scale(way, 2, scale))
-            values = chip_rows(1 + way, t, way) + z_values(way, 0, t)
-            z_piece(way, 2, t, values, factors[way])
-
-    gate_copy(1).wait_recv()
-    gate_copy(2).wait_recv()
+            values = chip_rows(1 + way, piece, way) + z_values(way, 0, piece)
+            zsend[way, 2, block(piece), :] = encoded(values, factors[way])
+            z_copy(way, 2, piece).start()
+
+    for which in range(3):
+        gate_copy(which).wait_recv()
     gate_total = ((gall[0] + gall[1]) + gall[2]) + gall[3]
     gshard[...] = (gate_total * (1 / 16)).astype(BF16)
 
-    def gate_send(i):
-        return pltpu.make_async_remote_copy(
+    pl.semaphore_wait(known.at[1], 1)
+    for peer in sa_peers:
+        pltpu.make_async_remote_copy(
             src_ref=gshard, dst_ref=out_gate.at[:, pl.ds(pl.multiple_of(sa * 128, 128), 128)],
             send_sem=ga_sem.at[0], recv_sem=ga_sem.at[1],
-            device_id=(row, (sa + i) % 32), device_id_type=MESH,
-        )
-
-    def gate_start(i, _):
-        gate_send(i).start()
-        return 0
-
-    pl.semaphore_wait(known.at[1], 1)
-    lax.fori_loop(1, 32, gate_start, 0)
+            device_id=(row, peer), device_id_type=MESH,
+        ).start()
     out_gate[:, pl.ds(pl.multiple_of(sa * 128, 128), 128)] = gshard[...]
 
     for t in range(3):
@@ -227,30 +235,27 @@
     norm_row = jnp.sum(rowsums[...].T, axis=0, keepdims=True)
     lane = lax.broadcasted_iota(jnp.int32, (1, 128), 1)
 
-    def msg_send(piece, i):
-        return pltpu.make_async_remote_copy(
-            src_ref=msgs.at[piece, (sa + i) % 32], dst_ref=recv.at[piece, sa],
-            send_sem=ms_sem.at[piece], recv_sem=mr_sem.at[piece],
-            device_id=(row, (sa + i) % 32), device_id_type=MESH,
-        )
-
     def send_all(piece):
-        def start(i, _):
-            msg_send(piece, i).start()
-            return 0
-
-        lax.fori_loop(1, 32, start, 0)
+        for peer in sa_peers:
+            pltpu.make_async_remote_copy(
+                src_ref=msgs.at[piece, peer], dst_ref=recv.at[piece, sa],
+                send_sem=ms_sem.at[piece], recv_sem=mr_sem.at[piece],
+                device_id=(row, peer), device_id_type=MESH,
+            ).start()
         recv[piece, sa] = msgs[piece, sa]
 
     d2d(3).wait_recv()
+    for way in range(2):
+        z_copy(way, 1, 0).wait_recv()
     for t in range(3):
-        for half in range(2):
-            total = chip_rows(3, t, half)
-            z_copy(1 - half, 1, t).wait_recv()
-            total = total + z_values(1 - half, 1, t)
-            z_copy(half, 2, t).wait_recv()
-            total = total + z_values(half, 2, t)
-            served[t, 64 * half : 64 * half + 64, :] = (total * (1 / 16)).astype(BF16).astype(F32)
+        for part in range(2):
+            for half in range(2):
+                piece = 2 * t + part
+                total = chip_rows(3, piece, half) + z_values(1 - half, 1, piece)
+                z_copy(half, 2, piece).wait_recv()
+                total = total + z_values(half, 2, piece)
+                start = 64 * half + BLOCK * part
+                served[t, start : start + BLOCK, :] = (total * (1 / 16)).astype(BF16).astype(F32)
         final = served[t]
         square = jnp.sum(final * final, axis=(0, 1), keepdims=True)
         norm_row = jnp.where(lane == 64 + t, square, norm_row)
@@ -271,9 +276,10 @@
     for k in range(4):
         d2d(k).wait_send()
     for way in range(2):
-        for stage in range(3):
-            for t in range(3):
-                z_copy(way, stage, t).wait_send()
+        z_copy(way, 1, 0).wait_send()
+        for stage in (0, 2):
+            for piece in range(6):
+                z_copy(way, stage, piece).wait_send()
     gate_d2d().wait_send()
     for which in range(3):
         gate_copy(which).wait_send()
@@ -338,8 +344,8 @@
             pltpu.VMEM((4, 392, 128), F32),
             pltpu.VMEM((384, 128), F32),
             pltpu.VMEM((128, 128), F32),
-            pltpu.VMEM((2, 3, 208, 128), BF16),
-            pltpu.VMEM((2, 3, 208, 128), BF16),
+            pltpu.VMEM((2, 3, FIRST + 192, 128), BF16),
+            pltpu.VMEM((2, 3, FIRST + 192, 128), BF16),
             pltpu.VMEM((5, 8, 128), F32),
             pltpu.VMEM((8, 128), F32),
             pltpu.VMEM((8, 128), BF16),
@@ -349,14 +355,14 @@
             dma,
             dma((4,)),
             dma((4,)),
-            dma((2, 3, 3)),
-            dma((2, 3, 3)),
+            dma((2, 3, 6)),
+            dma((2, 3, 6)),
             dma((2,)),
             dma((2, 3)),
             dma((2,)),
             dma((2,)),
             dma((2,)),
-            pltpu.SemaphoreType.REGULAR((2,)),
+            pltpu.SemaphoreType.REGULAR((3,)),
         ],
         compiler_params=pltpu.CompilerParams(collective_id=0, has_side_effects=True, vmem_limit_bytes=56 * 2**20),
     )(w1, w3, w2, gate)

time: 27.8 us -> 27.8 us (level)
  the two profiles are of different devices: /device:TPU:1 before, /device:TPU:2 now
where the time goes in v4:
time: 27.8 us; the launch traced here: 27.7 us
  Pallas kernels  27.1 us (97%)
  between operations  0.64 us (2%)
    pallas_call x1, Pallas kernels, body(): pl.pallas_call(kernel, name='soup', out_shape=(pltpu.VMEM((2, 32, 8, 128)...  26.3 us
    pallas_call x1, Pallas kernels, body(): pl.pallas_call(unpack, name='unpack', out_shape=(jax.ShapeDtypeStruct((1,...  0.73 us

profile of v4, /device:TPU:2, one launch (start us, length us, event | category | flops | bytes accessed | tf_op | source)
XLA Modules:
  0.0 27.7 jit_solution(17307521001804620246)
XLA Ops:
  0.6 26.3 %soup.1 = (bf16[2,32,8,128]{3,2,1,0:T(8,128)(2,1)S(1)}, bf16[8,4096]{1,0:T(8,128)(2,1)S(1)}) custom-call(f32[2,8,128,128]{3,2,1,0:T(8,128)} %w1.1, f32[2,8,128,128]{3,2,1,0:T(8,128)} %w3.1, f32[2,8,128,128]{3,2,1,0:T(8,128)} %w2.1, f32[2,8,128]{2,1,0:T(8,128)} %gate.1), custom_call_target="tpu_custom_call" | custom-call | tf_op jit(solution)/shard_map/soup/pallas_call | solution.py:330
  27.0 0.7 %unpack.1 = (bf16[1,4,4096]{2,1,0:T(4,128)(2,1)}, bf16[1,4,4096]{2,1,0:T(4,128)(2,1)}, bf16[1,4,4096]{2,1,0:T(4,128)(2,1)}, bf16[8,4096]{1,0:T(8,128)(2,1)}, f32[1,4]{1,0:T(1,128)}, /*index=5*/f32[2,4,8]{2,1,0:T(4,128)}) custom-call(bf16[2,32,8,128]{3,2,1,0:T(8,128)(2,1)S(1)} %get-tuple-element.14.recv, bf16[8,4096]{1,0:T(8,128)(2,1)S(1)} %get-tuple-element.15.gates), custom_call_target="tpu_custom_call" | custom-call | tf_op jit(solution)/shard_map/unpack/pallas_call | solution.py:369

commit v5 on v4

--- a/solution.py
+++ b/solution.py
@@ -142,9 +142,13 @@
         chunk_sums(k, 1 - core, dsend.at[k])
         if k == 0:
             pl.semaphore_wait(barrier, 10)
-            gate_d2d().start()
         d2d(k).start()
         if k == 0:
+
+            @pl.when(core == 0)
+            def _():
+                gate_d2d().start()
+
             pl.semaphore_signal(known.at[2], inc=1, device_id=(up, sa), device_id_type=MESH)
             for device in x_line:
                 pl.semaphore_signal(known.at[0], inc=1, device_id=device, device_id_type=MESH)
@@ -153,6 +157,12 @@
     def gate_d2d():
         return pltpu.make_async_remote_copy(
             src_ref=gall.at[4], dst_ref=gdrecv, send_sem=gd_sem.at[0], recv_sem=gd_sem.at[1],
+            device_id=(partner, sa), device_id_type=MESH,
+        )
+
+    def gate_over():
+        return pltpu.make_async_remote_copy(
+            src_ref=gshard, dst_ref=gshard, send_sem=gd_sem.at[2], recv_sem=gd_sem.at[3],
             device_id=(partner, sa), device_id_type=MESH,
         )
 
@@ -171,11 +181,9 @@
     prepare(0)
     prepare(1)
 
-    gate_d2d().wait_recv()
-    gall[zh] = gall[4] + gdrecv[...]
-    pl.semaphore_wait(known.at[2], 1)
-    for which in (2, 0, 1):
-        gate_copy(which).start()
+    @pl.when(core == 0)
+    def _():
+        pl.semaphore_wait(known.at[2], 1)
 
     d2d(0).wait_recv()
     scale = round_up(chip_top(0))
@@ -184,6 +192,16 @@
         for way in range(2):
             zsend[way, 0, block(piece), :] = encoded(chip_rows(0, piece, way), factors[way])
             z_copy(way, 0, piece).start()
+
+
+    @pl.when(core == 1)
+    def _():
+        pl.semaphore_wait(known.at[2], 1)
+        gate_d2d().wait_recv()
+        gall[zh] = gall[4] + gdrecv[...]
+        for which in (2, 0, 1):
+            gate_copy(which).start()
+
 
     prepare(2)
     pl.semaphore_wait(known.at[0], 3)
@@ -212,10 +230,18 @@
             zsend[way, 2, block(piece), :] = encoded(values, factors[way])
             z_copy(way, 2, piece).start()
 
-    for which in range(3):
-        gate_copy(which).wait_recv()
-    gate_total = ((gall[0] + gall[1]) + gall[2]) + gall[3]
-    gshard[...] = (gate_total * (1 / 16)).astype(BF16)
+    @pl.when(core == 1)
+    def _():
+        for which in range(3):
+            gate_copy(which).wait_recv()
+        gate_total = ((gall[0] + gall[1]) + gall[2]) + gall[3]
+        gshard[...] = (gate_total * (1 / 16)).astype(BF16)
+        gate_over().start()
+
+    @pl.when(core == 0)
+    def _():
+        gate_over().wait_recv()
+
 
     pl.semaphore_wait(known.at[1], 1)
     for peer in sa_peers:
@@ -280,9 +306,16 @@
         for stage in (0, 2):
             for piece in range(6):
                 z_copy(way, stage, piece).wait_send()
-    gate_d2d().wait_send()
-    for which in range(3):
-        gate_copy(which).wait_send()
+    @pl.when(core == 0)
+    def _():
+        gate_d2d().wait_send()
+
+    @pl.when(core == 1)
+    def _():
+        gate_over().wait_send()
+        for which in range(3):
+            gate_copy(which).wait_send()
+
     others = out_gate.at[:, pl.ds(0, 31 * 128)]
     pltpu.make_async_copy(others, others, ga_sem.at[0]).wait()
     pltpu.make_async_copy(others, others, ga_sem.at[1]).wait()
@@ -357,7 +390,7 @@
             dma((4,)),
             dma((2, 3, 6)),
             dma((2, 3, 6)),
-            dma((2,)),
+            dma((4,)),
             dma((2, 3)),
             dma((2,)),
             dma((2,)),

time: 27.8 us -> 27.2 us (0.978)
  Pallas kernels: 27.1 us -> 26.5 us
    pallas_call x1, Pallas kernels: 26.3 us -> 25.7 us  [body(): pl.pallas_call(kernel, name='soup', out_shape=(pltpu.VMEM((2, 32, 8, 128)...]
where the time goes in v5:
time: 27.2 us; the launch traced here: 27.1 us
  Pallas kernels  26.5 us (97%)
  between operations  0.64 us (2%)
    pallas_call x1, Pallas kernels, body(): pl.pallas_call(kernel, name='soup', out_shape=(pltpu.VMEM((2, 32, 8, 128)...  25.7 us
    pallas_call x1, Pallas kernels, body(): pl.pallas_call(unpack, name='unpack', out_shape=(jax.ShapeDtypeStruct((1,...  0.73 us

profile of v5, /device:TPU:2, one launch (start us, length us, event | category | flops | bytes accessed | tf_op | source)
XLA Modules:
  0.0 27.1 jit_solution(14655229871651228053)
XLA Ops:
  0.6 25.7 %soup.1 = (bf16[2,32,8,128]{3,2,1,0:T(8,128)(2,1)S(1)}, bf16[8,4096]{1,0:T(8,128)(2,1)S(1)}) custom-call(f32[2,8,128,128]{3,2,1,0:T(8,128)} %w1.1, f32[2,8,128,128]{3,2,1,0:T(8,128)} %w3.1, f32[2,8,128,128]{3,2,1,0:T(8,128)} %w2.1, f32[2,8,128]{2,1,0:T(8,128)} %gate.1), custom_call_target="tpu_custom_call" | custom-call | tf_op jit(solution)/shard_map/soup/pallas_call | solution.py:363
  26.4 0.7 %unpack.1 = (bf16[1,4,4096]{2,1,0:T(4,128)(2,1)}, bf16[1,4,4096]{2,1,0:T(4,128)(2,1)}, bf16[1,4,4096]{2,1,0:T(4,128)(2,1)}, bf16[8,4096]{1,0:T(8,128)(2,1)}, f32[1,4]{1,0:T(1,128)}, /*index=5*/f32[2,4,8]{2,1,0:T(4,128)}) custom-call(bf16[2,32,8,128]{3,2,1,0:T(8,128)(2,1)S(1)} %get-tuple-element.14.recv, bf16[8,4096]{1,0:T(8,128)(2,1)S(1)} %get-tuple-element.15.gates), custom_call_target="tpu_custom_call" | custom-call | tf_op jit(solution)/shard_map/unpack/pallas_call | solution.py:402

commit v6 on v5

--- a/solution.py
+++ b/solution.py
@@ -87,18 +87,21 @@
         for t in range(3):
             a, b = load[k, t, 0, parity], load[k, t, 1, parity]
             total = a + b
-            dest[t * 128 : (t + 1) * 128, :] = total
+            dest[8 + t * 128 : 136 + t * 128, :] = total
             for r, v in ((0, a), (1, b)):
                 index = pl.multiple_of((t * 16 + r * 8 + expert) * 8, 8)
                 squares[pl.ds(index, 8), :] = jnp.sum((v * v).reshape(16, 8, 128), axis=0)
             if k < 3:
                 top = jnp.maximum(top, jnp.max(jnp.abs(total).reshape(16, 8, 128), axis=0))
         if k < 3:
-            dest[384:392, :] = top
-
-    def d2d(k):
+            dest[0:8, :] = top
+
+    def d2d(k, rest=False):
+        rows = pl.ds(0, 392) if k else pl.ds(136, 256) if rest else pl.ds(0, 136)
+        slot = 4 if rest else k
         return pltpu.make_async_remote_copy(
-            src_ref=dsend.at[k], dst_ref=drecv.at[k], send_sem=ds_sem.at[k], recv_sem=dr_sem.at[k],
+            src_ref=dsend.at[k, rows], dst_ref=drecv.at[k, rows],
+            send_sem=ds_sem.at[slot], recv_sem=dr_sem.at[slot],
             device_id=(partner, sa), device_id_type=MESH,
         )
 
@@ -117,11 +120,11 @@
 
     def chip_rows(k, piece, half):
         t, part = piece // 2, piece % 2
-        start = t * 128 + half * 64 + part * BLOCK
+        start = 8 + t * 128 + half * 64 + part * BLOCK
         return sown[k, start : start + BLOCK, :] + drecv[k, start : start + BLOCK, :]
 
     def chip_top(k):
-        return row_max(sown[k, 384:392, :] + drecv[k, 384:392, :])
+        return row_max(sown[k, 0:8, :] + drecv[k, 0:8, :])
 
     def put_scale(way, stage, scale):
         zsend[way, stage, 0:FIRST, :] = jnp.broadcast_to(scale, (FIRST, 128))
@@ -144,6 +147,8 @@
             pl.semaphore_wait(barrier, 10)
         d2d(k).start()
         if k == 0:
+            d2d(0, True).start()
+        if k == 0:
 
             @pl.when(core == 0)
             def _():
@@ -189,6 +194,8 @@
     scale = round_up(chip_top(0))
     factors = [put_scale(way, 0, scale) for way in range(2)]
     for piece in range(6):
+        if piece == 2:
+            d2d(0, True).wait_recv()
         for way in range(2):
             zsend[way, 0, block(piece), :] = encoded(chip_rows(0, piece, way), factors[way])
             z_copy(way, 0, piece).start()
@@ -301,6 +308,7 @@
 
     for k in range(4):
         d2d(k).wait_send()
+    d2d(0, True).wait_send()
     for way in range(2):
         z_copy(way, 1, 0).wait_send()
         for stage in (0, 2):
@@ -386,8 +394,8 @@
             pltpu.VMEM((2, 32, 8, 128), BF16),
             dma((4, 3)),
             dma,
-            dma((4,)),
-            dma((4,)),
+            dma((5,)),
+            dma((5,)),
             dma((2, 3, 6)),
             dma((2, 3, 6)),
             dma((4,)),

time: 27.2 us -> 26.8 us (0.985)
  Pallas kernels: 26.5 us -> 26.1 us
    pallas_call x1, Pallas kernels: 25.7 us -> 25.4 us  [body(): pl.pallas_call(kernel, name='soup', out_shape=(pltpu.VMEM((2, 32, 8, 128)...]
where the time goes in v6:
time: 26.8 us; the launch traced here: 26.7 us
  Pallas kernels  26.1 us (97%)
  between operations  0.64 us (2%)
    pallas_call x1, Pallas kernels, body(): pl.pallas_call(kernel, name='soup', out_shape=(pltpu.VMEM((2, 32, 8, 128)...  25.4 us
    pallas_call x1, Pallas kernels, body(): pl.pallas_call(unpack, name='unpack', out_shape=(jax.ShapeDtypeStruct((1,...  0.73 us

profile of v6, /device:TPU:2, one launch (start us, length us, event | category | flops | bytes accessed | tf_op | source)
XLA Modules:
  0.0 26.7 jit_solution(15149026186172101416)
XLA Ops:
  0.6 25.4 %soup.1 = (bf16[2,32,8,128]{3,2,1,0:T(8,128)(2,1)S(1)}, bf16[8,4096]{1,0:T(8,128)(2,1)S(1)}) custom-call(f32[2,8,128,128]{3,2,1,0:T(8,128)} %w1.1, f32[2,8,128,128]{3,2,1,0:T(8,128)} %w3.1, f32[2,8,128,128]{3,2,1,0:T(8,128)} %w2.1, f32[2,8,128]{2,1,0:T(8,128)} %gate.1), custom_call_target="tpu_custom_call" | custom-call | tf_op jit(solution)/shard_map/soup/pallas_call | solution.py:371
  26.0 0.7 %unpack.1 = (bf16[1,4,4096]{2,1,0:T(4,128)(2,1)}, bf16[1,4,4096]{2,1,0:T(4,128)(2,1)}, bf16[1,4,4096]{2,1,0:T(4,128)(2,1)}, bf16[8,4096]{1,0:T(8,128)(2,1)}, f32[1,4]{1,0:T(1,128)}, /*index=5*/f32[2,4,8]{2,1,0:T(4,128)}) custom-call(bf16[2,32,8,128]{3,2,1,0:T(8,128)(2,1)S(1)} %get-tuple-element.14.recv, bf16[8,4096]{1,0:T(8,128)(2,1)S(1)} %get-tuple-element.15.gates), custom_call_target="tpu_custom_call" | custom-call | tf_op jit(solution)/shard_map/unpack/pallas_call | solution.py:410
